TPU v7x, 32 devices: a whole 2x2x4 slice. The times are simulated.
32 devices in a mesh: ga: 8 (over z, x), band: 4 (over y, core).
Axes of the slice: x: 2, y: 2, z: 4, core: 2. Of those that a mesh axis runs over, the one named last changes fastest.
Arguments:
- coeffs: bfloat16 [2, 512, 40960], P(None, ('ga', 'band')), may hold values from -6 to 6
- projectors: bfloat16 [1280, 2, 40960], P(None, None, 'ga'), may hold values from -0.01953125 to 0.01953125
- block_coupling: float32 [1280, 18], replicated, may hold values from -12 to 12
- atom_counts: int32 [160], replicated, may hold values from 4 to 18, as said below
- wave_counts: int32 [8], P('ga'), may hold values from 3840 to 5120
Outputs:
- applied: bfloat16 [2, 512, 40960], P(None, ('ga', 'band'))
- band_energy: float32 [512], P(('ga', 'band'))
- total_energy: float32 [], replicated
Inputs may be any that keep to these rules, and one draw needn't show every extreme that they name: `atom_counts`: each atom has 4, 8 or 18 projectors, the counts sum to 1280 and the largest is 18.
All inputs are finite; a program needn't handle non-finite values.
Results may differ from a plain program's by a relative error of at most 0.013.
Values may be sent and summed in bfloat16 or wider, within the bound.
A program may use at most 128 MiB of HBM per device.

v0:
```python
import math
import jax
import jax.numpy as jnp
from jax import lax
from jax.sharding import PartitionSpec as P


def block_tables(atom_counts, row_ids):
    atom_ends = jnp.cumsum(atom_counts)
    atom_starts = atom_ends - atom_counts
    inside = (atom_starts[None, :] <= row_ids[:, None]) & (atom_ends[None, :] > row_ids[:, None])
    block_first = jnp.sum(jnp.where(inside, atom_starts[None, :], 0), axis=1)
    block_length = jnp.sum(jnp.where(inside, atom_counts[None, :], 0), axis=1)
    return (block_first, block_length)


def coupling_matrix(block_first, block_length, coupling_rows, column_count):
    column_ids = lax.iota(jnp.int32, column_count)
    offsets = column_ids[None, :] - block_first[:, None]
    matrix = jnp.zeros((coupling_rows.shape[0], column_count), jnp.float32)
    for offset in range(coupling_rows.shape[1]):
        hit = (offsets == offset) & (offset < block_length[:, None])
        matrix = jnp.where(hit, coupling_rows[:, offset : offset + 1], matrix)
    return matrix


def shards(coeffs, projectors, block_coupling, atom_counts, wave_counts):
    moved_bands = lax.all_to_all(coeffs, "ga", split_axis=2, concat_axis=1, tiled=True)
    own_bands = coeffs.shape[1]
    group_bands = moved_bands.shape[1]
    wave_slots = projectors.shape[2]
    proj_total_rows = projectors.shape[0]
    in_sphere = (lax.iota(jnp.int32, wave_slots) < wave_counts[0]).astype(jnp.float32)
    masked = moved_bands * in_sphere.astype(jnp.bfloat16)
    real_part = masked[0]
    imag_part = masked[1]
    stacked = jnp.concatenate(
        [jnp.concatenate([real_part, imag_part], 1), jnp.concatenate([imag_part, -real_part], 1)], 0
    )
    flat_beta = projectors.reshape(proj_total_rows, 2 * wave_slots)
    contract_last = (((1,), (1,)), ((), ()))
    contract_first = (((0,), (0,)), ((), ()))
    ga_index = lax.axis_index("ga")
    local_terms = lax.dot_general(
        flat_beta, stacked, contract_last, preferred_element_type=jnp.float32
    )
    projections = lax.psum(local_terms, "ga")
    block_first, block_length = block_tables(atom_counts, lax.iota(jnp.int32, proj_total_rows))
    matrix = coupling_matrix(block_first, block_length, block_coupling, proj_total_rows)
    coupled = jnp.dot(
        matrix, projections, precision=lax.Precision.HIGHEST, preferred_element_type=jnp.float32
    )
    energy_terms = jnp.sum(projections * coupled, axis=0)
    group_energy = (energy_terms[:group_bands] + energy_terms[group_bands:]) / proj_total_rows
    band_energy = lax.dynamic_slice_in_dim(group_energy, ga_index * own_bands, own_bands, 0)
    total_energy = lax.psum(jnp.sum(group_energy), "band")
    products = lax.dot_general(
        coupled.astype(jnp.bfloat16), flat_beta, contract_first, preferred_element_type=jnp.float32
    )
    band_total = own_bands * lax.axis_size("ga") * lax.axis_size("band")
    total_energy = total_energy / math.sqrt(band_total)
    real_out = products[:group_bands, :wave_slots] - products[group_bands:, wave_slots:]
    imag_out = products[:group_bands, wave_slots:] + products[group_bands:, :wave_slots]
    result = (jnp.stack([real_out, imag_out]) * in_sphere).astype(jnp.bfloat16)
    applied = lax.all_to_all(result, "ga", split_axis=1, concat_axis=2, tiled=True)
    return (applied, band_energy, total_energy)


def solution(mesh):
    placed = (P(None, ("ga", "band"), None), P(None, None, "ga"), P(), P(), P("ga"))
    return jax.shard_map(
        shards,
        mesh=mesh,
        in_specs=placed,
        out_specs=(P(None, ("ga", "band"), None), P(("ga", "band")), P()),
        check_vma=False,
    )
```

profile of v0, /device:TPU:0, one launch (start us, length us, event | category | flops | bytes accessed | tf_op | source)
XLA Modules:
  0.0 439.4 jit_solution(13984395675737779399)
XLA Ops:
  7.2 38.0 %copy.21 = bf16[2,16,40960]{1,0,2:T(2,128)(2,1)} copy(bf16[2,16,40960]{2,1,0:T(8,128)(2,1)} %param.5) | data formatting | bytes 5242880 | tf_op args[0]
  45.1 24.1 %reshape.129 = bf16[8,2,81920]{2,1,0:T(2,128)(2,1)} reshape(bf16[40960,2,16]{2,1,0:T(2,128)(2,1)} %bitcast.40) | data formatting | bytes 5242880
  69.2 7.3 %all-to-all-start = ((bf16[8,2,81920]{2,1,0:T(2,128)(2,1)}), bf16[8,2,81920]{2,1,0:T(2,128)(2,1)S(1)}, u32[]{:S(2)}, u32[]{:S(2)}) async-start(bf16[8,2,81920]{2,1,0:T(2,128)(2,1)} %reshape.129), calls=%async_computation | async-start | bytes 5242880 | tf_op jit(solution)/shard_map/all_to_all | solution.py:28
  76.5 0.4 all-reduce.3.cloned.1.call-start
  77.6 23.8 %copy.29 = bf16[160,8,2,5120]{3,1,2,0:T(8,128)(2,1)} copy(bf16[160,8,2,5120]{3,2,1,0:T(2,128)(2,1)} %bitcast.41) | data formatting | bytes 52428800
  101.3 34.6 %all-to-all-done = bf16[8,2,81920]{2,1,0:T(2,128)(2,1)S(1)} async-done(((bf16[8,2,81920]{2,1,0:T(2,128)(2,1)}), bf16[8,2,81920]{2,1,0:T(2,128)(2,1)S(1)}, u32[]{:S(2)}, u32[]{:S(2)}) %all-to-all-start) | async-done | bytes 2621472 | tf_op jit(solution)/shard_map/all_to_all | solution.py:28
  136.0 17.1 %reshape.130 = bf16[40960,2,16]{2,1,0:T(2,128)(2,1)} reshape(bf16[8,2,81920]{2,1,0:T(2,128)(2,1)S(1)} %all-to-all-done) | data formatting | bytes 5242880
  153.0 37.5 %copy.28 = bf16[2,16,8,5120]{3,1,2,0:T(8,128)(2,1)S(1)} copy(bf16[2,16,8,5120]{1,0,3,2:T(2,128)(2,1)} %bitcast.39) | data formatting | bytes 5242880 | tf_op jit(solution)/shard_map/all_to_all | solution.py:28
  190.5 0.3 bitcast_multiply_fusion
  190.9 0.2 slice_bitcast_fusion.1
  191.1 0.1 fusion.168
  191.2 0.0 copy-start.1
  191.2 0.0 copy-start
  191.2 28.8 %fusion.138 = f32[1280,256]{0,1:T(8,128)} fusion(bf16[1280,10240]{1,0:T(8,128)(2,1)} %bitcast.37, bf16[128,5120]{1,0:T(8,128)(2,1)S(1)} %fusion.168, bf16[128,5120]{1,0:T(8,128)(2,1)S(1)} %get-tuple-element.28, bf16[128,5120]{1,0:T(8,128)(2,1)S(1)} %get-tuple-element.27), kind=kOutput, calls=%fused_computation.122 | convolution fusion | flops 6731857920 | bytes 31457280 | tf_op jit(solution)/shard_map/dot_general | solution.py:44
  220.0 0.0 all-reduce.3.cloned.1.call-update
  220.1 0.0 copy-done.1
  220.1 0.3 reduce-window.9
  220.4 0.1 slice.88
  220.5 0.1 slice_reduce_fusion.18
  220.6 0.0 copy-done
  220.6 0.2 slice_reduce_fusion.17
  220.9 0.1 add_bitcast_fusion
  220.9 0.3 select_reduce_fusion
  221.3 81.6 %all-reduce.3.cloned.1.call-done = f32[1280,256]{0,1:T(8,128)} async-done(((f32[1280,256]{0,1:T(8,128)}), f32[1280,256]{0,1:T(8,128)}) %all-reduce.3.cloned.1.call-update) | async-done | bytes 1310736 | tf_op jit(solution)/shard_map/psum | solution.py:47
  303.0 39.1 %fusion = f32[1280,256]{1,0:T(8,128)} fusion(f32[1280,256]{0,1:T(8,128)} %all-reduce.3.cloned.1.call-done, f32[1280]{0:T(1024)S(1)} %get-tuple-element.19, f32[1280]{0:T(1024)S(1)} %get-tuple-element.20, f32[1280]{0:T(1024)S(1)} %get-tuple-element.4, f32[1280]{0:T(1024)S(1)} %get-tuple-element.5, f32[1280]{0:T(1024)S(1)} %get-tuple-element.6, ...), kind=kOutput, calls=%fused_computation | convolution fusion | flops 5123276800 | bytes 2741760 | tf_op jit(solution)/shard_map/dot_general | solution.py:50
  342.1 13.0 %fusion.144 = f32[256,10240]{1,0:T(8,128)S(1)} fusion(bf16[1280,10240]{1,0:T(8,128)(2,1)} %bitcast.38, f32[1280,256]{1,0:T(8,128)} %fusion), kind=kOutput, calls=%fused_computation.136 | convolution fusion | flops 6711214080 | bytes 38010880 | tf_op jit(solution)/shard_map/dot_general | solution.py:57
  355.1 0.8 fusion.142
  355.9 0.5 fusion.81
  356.4 4.2 copy.24
  360.6 3.7 all-to-all-start.1
  364.2 2.8 copy.26
  367.0 1.9 multiply_reduce_fusion
  368.9 0.6 fusion.169
  369.5 7.3 %psum.15 = f32[]{:T(128)} all-reduce(f32[]{:T(128)} %get-tuple-element.23), channel_id=1, replica_groups=mesh['ga'=8,'band'=4] {'band'}, use_global_device_ids=true, to_apply=%region_7.8 | all-reduce | flops 1 | bytes 8 | tf_op jit(solution)/shard_map/psum | solution.py:56
  376.9 0.6 dynamic_slice.3
  378.1 45.7 %all-to-all-done.1 = bf16[2,128,5120]{2,0,1:T(2,128)(2,1)S(1)} async-done(((bf16[2,128,5120]{2,0,1:T(2,128)(2,1)}), bf16[2,128,5120]{2,0,1:T(2,128)(2,1)S(1)}, u32[]{:S(2)}, u32[]{:S(2)}) %all-to-all-start.1) | async-done | bytes 2621472 | tf_op jit(solution)/shard_map/all_to_all | solution.py:65
  423.8 2.9 copy.25
  426.7 4.5 %all_to_all.33 = bf16[2,16,40960]{2,1,0:T(8,128)(2,1)} reshape(bf16[2,16,8,5120]{3,2,1,0:T(8,128)(2,1)} %copy.25) | data formatting | bytes 5242880 | tf_op jit(solution)/shard_map/all_to_all | solution.py:65
  (5 shorter events, 0.1 us)
Async XLA Ops:
  69.2 66.8 %all-to-all-start = ((bf16[8,2,81920]{2,1,0:T(2,128)(2,1)}), bf16[8,2,81920]{2,1,0:T(2,128)(2,1)S(1)}, u32[]{:S(2)}, u32[]{:S(2)}) async-start(bf16[8,2,81920]{2,1,0:T(2,128)(2,1)} %reshape.129), calls=%async_computation | async-start | bytes 5242880 | tf_op jit(solution)/shard_map/all_to_all | solution.py:28
  76.5 226.5 %all-reduce.3.cloned.1.call-start = ((), (), s32[]{:S(2)}) async-start(), calls=%async_computation.2 | async-start | bytes 2621440 | tf_op jit(solution)/shard_map/psum | solution.py:47
  191.2 28.9 %copy-start.1 = (s32[160]{0:T(256)S(1)}, s32[160]{0:T(256)}, u32[]{:S(2)}) copy-start(s32[160]{0:T(256)} %param.8) | copy-start | bytes 1924
  191.2 29.4 %copy-start = (f32[1280,18]{0,1:T(8,128)S(1)}, f32[1280,18]{0,1:T(8,128)}, u32[]{:S(2)}) copy-start(f32[1280,18]{0,1:T(8,128)} %param.7) | copy-start | bytes 276484
  360.6 63.2 %all-to-all-start.1 = ((bf16[2,128,5120]{2,0,1:T(2,128)(2,1)}), bf16[2,128,5120]{2,0,1:T(2,128)(2,1)S(1)}, u32[]{:S(2)}, u32[]{:S(2)}) async-start(bf16[2,128,5120]{2,0,1:T(2,128)(2,1)} %copy.24), calls=%async_computation.1 | async-start | bytes 5242880 | tf_op jit(solution)/shard_map/all_to_all | solution.py:65
Sparse Core Ops, SparseCore 0:
  220.2 82.7 all-reduce.2
where the time goes:
time: 447 us; the launch traced here: 439 us
  waiting for transfers between devices  162 us (36%)
  local copies, waits for them, and re-layouts  156 us (35%)
  matrix products  81 us (18%)
  between operations  16.8 us (4%)
  starting transfers between devices  11.4 us (3%)
  blocking collectives  7.33 us (2%)
  other arithmetic  4.94 us (1%)
    unnamed x8, local copies, waits for them, and re-layouts  103 us
    psum x1, waiting for transfers between devices, shards(): projections = lax.psum(local_terms, 'ga')  81.6 us
    all_to_all x1, waiting for transfers between devices, shards(): lax.all_to_all(result, 'ga', split_axis=1, concat_axis=2, tiled=True)  45.7 us
    dot_general x1, matrix products, shards(): jnp.dot(matrix, projections, precision=lax.Precision.HIGHEST, preferred_e...  39.1 us
    all_to_all x1, local copies, waits for them, and re-layouts, shards(): lax.all_to_all(coeffs, 'ga', split_axis=2, concat_axis=1, tiled=True)  37.5 us
    all_to_all x1, waiting for transfers between devices, shards(): lax.all_to_all(coeffs, 'ga', split_axis=2, concat_axis=1, tiled=True)  34.6 us
    dot_general x1, matrix products, shards(): lax.dot_general(flat_beta, stacked, contract_last, preferred_element_type...  28.8 us
    dot_general x1, matrix products, shards(): lax.dot_general(coupled.astype(jnp.bfloat16), flat_beta, contract_first,...  13 us
  transfers between devices with their start and end apart: 3, of which 3 were waited for; matrix products, arithmetic and copies ran while one was open for 7% of the time, Pallas kernels for 0%

commit v1 on v0

--- a/solution.py
+++ b/solution.py
@@ -44,7 +44,7 @@
     local_terms = lax.dot_general(
         flat_beta, stacked, contract_last, preferred_element_type=jnp.float32
     )
-    projections = lax.psum(local_terms, "ga")
+    projections = jnp.sum(lax.all_gather(local_terms, "ga"), axis=0)
     block_first, block_length = block_tables(atom_counts, lax.iota(jnp.int32, proj_total_rows))
     matrix = coupling_matrix(block_first, block_length, block_coupling, proj_total_rows)
     coupled = jnp.dot(

time: 447 us -> 515 us (1.15)
  waiting for transfers between devices: 162 us -> 234 us
  matrix products: 81 us -> 70.1 us
  local copies, waits for them, and re-layouts: 156 us -> 163 us
    all_gather x0 -> x1, waiting for transfers between devices: none -> 148 us  [shards(): projections = jnp.sum(lax.all_gather(local_terms, 'ga'), axis=0)]
    psum x1 -> x0, waiting for transfers between devices: 81.6 us -> none  [shards(): projections = lax.psum(local_terms, 'ga')]
    dot_general x1, matrix products: 39.1 us -> 28.7 us  [shards(): jnp.dot(matrix, projections, precision=lax.Precision.HIGHEST, preferred_e...]
    unnamed x8 -> x9, local copies, waits for them, and re-layouts: 103 us -> 111 us
  transfers between devices with their start and end apart: 3 -> 3, of which waited for: 3 -> 3; matrix products, arithmetic and copies ran while one was open for 7% -> 5% of each run, Pallas kernels for 0% -> 0%
where the time goes in v1:
time: 515 us; the launch traced here: 507 us
  waiting for transfers between devices  234 us (45%)
  local copies, waits for them, and re-layouts  163 us (32%)
  matrix products  70.1 us (14%)
  between operations  16.8 us (3%)
  starting transfers between devices  11.2 us (2%)
  blocking collectives  6.75 us (1%)
  other arithmetic  5.33 us (1%)
    all_gather x1, waiting for transfers between devices, shards(): projections = jnp.sum(lax.all_gather(local_terms, 'ga'), axis=0)  148 us
    unnamed x9, local copies, waits for them, and re-layouts  111 us
    all_to_all x1, waiting for transfers between devices, shards(): lax.all_to_all(result, 'ga', split_axis=1, concat_axis=2, tiled=True)  50.4 us
    all_to_all x1, local copies, waits for them, and re-layouts, shards(): lax.all_to_all(coeffs, 'ga', split_axis=2, concat_axis=1, tiled=True)  37.5 us
    all_to_all x1, waiting for transfers between devices, shards(): lax.all_to_all(coeffs, 'ga', split_axis=2, concat_axis=1, tiled=True)  34.7 us
    dot_general x1, matrix products, shards(): lax.dot_general(flat_beta, stacked, contract_last, preferred_element_type...  29.3 us
    dot_general x1, matrix products, shards(): jnp.dot(matrix, projections, precision=lax.Precision.HIGHEST, preferred_e...  28.7 us
    dot_general x1, matrix products, shards(): lax.dot_general(coupled.astype(jnp.bfloat16), flat_beta, contract_first,...  12.1 us
  transfers between devices with their start and end apart: 3, of which 3 were waited for; matrix products, arithmetic and copies ran while one was open for 5% of the time, Pallas kernels for 0%

profile of v1, /device:TPU:0, one launch (start us, length us, event | category | flops | bytes accessed | tf_op | source)
XLA Modules:
  0.0 506.9 jit_solution(8275240517535720569)
XLA Ops:
  7.2 38.0 %copy.18 = bf16[2,16,40960]{1,0,2:T(2,128)(2,1)} copy(bf16[2,16,40960]{2,1,0:T(8,128)(2,1)} %param.5) | data formatting | bytes 5242880 | tf_op args[0]
  45.1 24.1 %reshape.130 = bf16[8,2,81920]{2,1,0:T(2,128)(2,1)} reshape(bf16[40960,2,16]{2,1,0:T(2,128)(2,1)} %bitcast.46) | data formatting | bytes 5242880
  69.2 7.3 %all-to-all-start = ((bf16[8,2,81920]{2,1,0:T(2,128)(2,1)}), bf16[8,2,81920]{2,1,0:T(2,128)(2,1)S(1)}, u32[]{:S(2)}, u32[]{:S(2)}) async-start(bf16[8,2,81920]{2,1,0:T(2,128)(2,1)} %reshape.130), calls=%async_computation | async-start | bytes 5242880 | tf_op jit(solution)/shard_map/all_to_all | solution.py:28
  76.5 0.3 all-gather.3.cloned.1.call-start
  77.5 23.8 %copy.26 = bf16[160,8,2,5120]{3,1,2,0:T(8,128)(2,1)} copy(bf16[160,8,2,5120]{3,2,1,0:T(2,128)(2,1)} %bitcast.47) | data formatting | bytes 52428800
  101.3 34.7 %all-to-all-done = bf16[8,2,81920]{2,1,0:T(2,128)(2,1)S(1)} async-done(((bf16[8,2,81920]{2,1,0:T(2,128)(2,1)}), bf16[8,2,81920]{2,1,0:T(2,128)(2,1)S(1)}, u32[]{:S(2)}, u32[]{:S(2)}) %all-to-all-start) | async-done | bytes 2621472 | tf_op jit(solution)/shard_map/all_to_all | solution.py:28
  136.0 17.1 %reshape.131 = bf16[40960,2,16]{2,1,0:T(2,128)(2,1)} reshape(bf16[8,2,81920]{2,1,0:T(2,128)(2,1)S(1)} %all-to-all-done) | data formatting | bytes 5242880
  153.0 37.5 %copy.25 = bf16[2,16,8,5120]{3,1,2,0:T(8,128)(2,1)S(1)} copy(bf16[2,16,8,5120]{1,0,3,2:T(2,128)(2,1)} %bitcast.45) | data formatting | bytes 5242880 | tf_op jit(solution)/shard_map/all_to_all | solution.py:28
  190.5 0.3 bitcast_multiply_fusion
  190.9 0.2 slice_bitcast_fusion.1
  191.1 0.1 fusion.168
  191.2 0.0 copy-start.1
  191.2 0.0 copy-start
  191.2 29.3 %fusion.138 = f32[1280,256]{0,1:T(8,128)} fusion(bf16[1280,10240]{1,0:T(8,128)(2,1)} %bitcast.43, bf16[128,5120]{1,0:T(8,128)(2,1)S(1)} %fusion.168, bf16[128,5120]{1,0:T(8,128)(2,1)S(1)} %get-tuple-element.28, bf16[128,5120]{1,0:T(8,128)(2,1)S(1)} %get-tuple-element.27), kind=kOutput, calls=%fused_computation.123 | convolution fusion | flops 6731857920 | bytes 31457280 | tf_op jit(solution)/shard_map/dot_general | solution.py:44
  220.5 0.0 all-gather.3.cloned.1.call-update
  220.6 0.0 copy-done.1
  220.6 0.3 reduce-window.9
  220.9 0.1 slice.88
  221.0 0.1 slice_reduce_fusion.18
  221.1 0.0 copy-done
  221.1 0.3 slice_reduce_fusion.17
  221.4 0.1 add_bitcast_fusion
  221.5 0.3 select_reduce_fusion
  221.8 148.5 %all-gather.3.cloned.1.call-done = f32[10240,256]{0,1:T(8,128)} async-done(((f32[1280,256]{0,1:T(8,128)}), f32[10240,256]{0,1:T(8,128)}) %all-gather.3.cloned.1.call-update) | async-done | bytes 10485776 | tf_op jit(solution)/shard_map/all_gather | solution.py:47
  370.3 8.3 %copy.27 = f32[32,8,8,1280]{3,2,1,0:T(8,128)S(1)} copy(f32[32,8,8,1280]{3,1,2,0:T(8,128)} %bitcast.48) | data formatting | bytes 20971520
  378.6 2.5 bitcast_reduce_fusion
  381.1 1.5 copy.23
  382.5 28.7 %multiply_reduce_fusion = (f32[256]{0:T(256)S(1)}, bf16[1280,256]{1,0:T(8,128)(2,1)S(1)}) fusion(f32[1280,256]{1,0:T(8,128)} %copy.23, f32[1280,256]{0,1:T(8,128)S(1)} %bitcast_reduce_fusion, f32[1280]{0:T(1024)S(1)} %get-tuple-element.19, f32[1280]{0:T(1024)S(1)} %get-tuple-element.20, f32[1280]{0:T(1024)S(1)} %get-tuple-element.4, ...), kind=kOutput, calls=%fused_computation.131 | convolution fusion | flops 5124259840 | bytes 3398144 | tf_op jit(solution)/shard_map/dot_general | solution.py:50
  411.2 12.1 %fusion.144 = f32[256,10240]{1,0:T(8,128)S(1)} fusion(bf16[1280,10240]{1,0:T(8,128)(2,1)} %bitcast.44, bf16[1280,256]{1,0:T(8,128)(2,1)S(1)} %get-tuple-element.50), kind=kOutput, calls=%fused_computation.137 | convolution fusion | flops 6710886400 | bytes 37355520 | tf_op jit(solution)/shard_map/dot_general | solution.py:57
  423.4 0.6 fusion.142
  424.0 0.5 fusion.81
  424.4 4.2 copy.21
  428.6 3.6 all-to-all-start.1
  432.3 0.6 fusion.169
  432.9 6.7 %psum.7 = f32[]{:T(128)} all-reduce(f32[]{:T(128)} %get-tuple-element.23), channel_id=1, replica_groups=mesh['ga'=8,'band'=4] {'band'}, use_global_device_ids=true, to_apply=%region_7.8 | all-reduce | flops 1 | bytes 8 | tf_op jit(solution)/shard_map/psum | solution.py:56
  439.6 0.6 dynamic_slice.3
  440.8 50.4 %all-to-all-done.1 = bf16[2,128,5120]{2,0,1:T(2,128)(2,1)S(1)} async-done(((bf16[2,128,5120]{2,0,1:T(2,128)(2,1)}), bf16[2,128,5120]{2,0,1:T(2,128)(2,1)S(1)}, u32[]{:S(2)}, u32[]{:S(2)}) %all-to-all-start.1) | async-done | bytes 2621472 | tf_op jit(solution)/shard_map/all_to_all | solution.py:65
  491.2 2.9 copy.22
  494.2 4.5 all_to_all.33
  (5 shorter events, 0.1 us)
Async XLA Ops:
  69.2 66.8 %all-to-all-start = ((bf16[8,2,81920]{2,1,0:T(2,128)(2,1)}), bf16[8,2,81920]{2,1,0:T(2,128)(2,1)S(1)}, u32[]{:S(2)}, u32[]{:S(2)}) async-start(bf16[8,2,81920]{2,1,0:T(2,128)(2,1)} %reshape.130), calls=%async_computation | async-start | bytes 5242880 | tf_op jit(solution)/shard_map/all_to_all | solution.py:28
  76.5 293.8 %all-gather.3.cloned.1.call-start = ((), (), s32[]{:S(2)}) async-start(), calls=%async_computation.2 | async-start | bytes 11796480 | tf_op jit(solution)/shard_map/all_gather | solution.py:47
  191.2 29.4 %copy-start.1 = (s32[160]{0:T(256)S(1)}, s32[160]{0:T(256)}, u32[]{:S(2)}) copy-start(s32[160]{0:T(256)} %param.8) | copy-start | bytes 1924
  191.2 29.9 %copy-start = (f32[1280,18]{0,1:T(8,128)S(1)}, f32[1280,18]{0,1:T(8,128)}, u32[]{:S(2)}) copy-start(f32[1280,18]{0,1:T(8,128)} %param.7) | copy-start | bytes 276484
  428.6 62.6 %all-to-all-start.1 = ((bf16[2,128,5120]{2,0,1:T(2,128)(2,1)}), bf16[2,128,5120]{2,0,1:T(2,128)(2,1)S(1)}, u32[]{:S(2)}, u32[]{:S(2)}) async-start(bf16[2,128,5120]{2,0,1:T(2,128)(2,1)} %copy.21), calls=%async_computation.1 | async-start | bytes 5242880 | tf_op jit(solution)/shard_map/all_to_all | solution.py:65
Sparse Core Ops, SparseCore 0:
  220.7 149.5 all-gather.2
